TPU v7x, 32 devices: a whole 2x2x4 slice. The times are simulated.
32 devices in a mesh: replica: 8 (over z, y), shard: 4 (over x, core).
Axes of the slice: x: 2, y: 2, z: 4, core: 2. Of those that a mesh axis runs over, the one named last changes fastest.
Arguments:
- outer_params: float32 [512, 4096], P('shard'), may hold values from -6 to 6, as said below
- local_params: bfloat16 [8, 512, 4096], P('replica', 'shard'), may hold values from -70 to 70
- momentum: float32 [512, 4096], P('shard'), may hold values from -6 to 6
Outputs:
- params_next: float32 [512, 4096], P('shard')
- momentum_next: float32 [512, 4096], P('shard')
- block_scales: float32 [32, 512], P(None, 'shard')
Inputs may be any that keep to these rules, and one draw needn't show every extreme that they name: `outer_params`: outer parameters of order one.
All inputs are finite; a program needn't handle non-finite values.
Results may differ from a plain program's by a relative error of at most 0.005.
Values may be sent and summed in bfloat16 or wider, within the bound.
A program may use at most 64 MiB of HBM per device.

v0:
```python
import functools

import jax
import jax.numpy as jnp
from jax import lax
from jax.experimental import pallas as pl
from jax.experimental.pallas import tpu as pltpu
from jax.sharding import PartitionSpec as P

BLOCK = 128
MESH = pl.DeviceIdType.MESH

epsilon = 1e-06
clip_level = 0.5
outer_rate = 0.7
outer_decay = 0.9
grid_levels = 7.0

SMOOTH = (6.57973588, -12.98785441, 12.20756634, -6.687892761, 2.368806331, -0.5120006377)
SHIFT = 1.5 * 2.0**23


def smooth_rest(rest):
    square = rest * rest
    value = SMOOTH[-1]
    for coefficient in SMOOTH[-2::-1]:
        value = value * square + coefficient
    return rest * square * value


def column_of(row):
    return jnp.broadcast_to(row, (BLOCK, row.shape[1])).T


def exchange_kernel(
    workers, shards, entry_count,
    outer_hbm, local_hbm, momentum_hbm, grad_out, momentum_out, max_out, factor_out,
    outer_v, local_v, max_slots, inverse, spread, encoded, arrived, total, share, squares, shard_squares,
    load_sem, max_send, max_recv, enc_send, enc_recv, sq_send, sq_recv, ss_send, ss_recv, gat_send, gat_recv, fwd_send, fwd_recv, own_sem, momentum_sem,
):
    me = lax.axis_index("replica")
    my_shard = lax.axis_index("shard")
    rows, cols = outer_v.shape
    blocks = cols // BLOCK
    width = cols // workers
    blocks_each = width // BLOCK
    parts, half = share.shape[:2]
    pieces = load_sem.shape[1]
    piece = cols // pieces

    def peer(step):
        return lax.rem(me + step, workers)

    def origin(step):
        return lax.rem(me + workers - step, workers)

    def loads(i):
        part = pl.ds(i * piece, piece)
        return (
            pltpu.make_async_copy(outer_hbm.at[:, part], outer_v.at[:, part], load_sem.at[0, i]),
            pltpu.make_async_copy(local_hbm.at[0, :, part], local_v.at[:, part], load_sem.at[1, i]),
        )

    for i in range(pieces):
        for copy in loads(i):
            copy.start()
    momentum_copy = pltpu.make_async_copy(momentum_hbm, momentum_out, momentum_sem)

    barrier = pltpu.get_barrier_semaphore()

    @pl.loop(1, workers)
    def _(step):
        pl.semaphore_signal(barrier, inc=1, device_id={"replica": peer(step)}, device_id_type=MESH)

    @pl.loop(1, shards)
    def _(step):
        pl.semaphore_signal(
            barrier, inc=1, device_id={"shard": lax.rem(my_shard + step, shards)}, device_id_type=MESH
        )

    def delta(block, rows_at=slice(None)):
        at = pl.ds(pl.multiple_of(block * BLOCK, BLOCK), BLOCK)
        return outer_v[rows_at, at] - local_v[rows_at, at].astype(jnp.float32)

    per_piece = piece // BLOCK

    def max_copy(i, step):
        mine = max_slots.at[me, pl.ds(i * per_piece, per_piece)]
        return pltpu.make_async_remote_copy(
            src_ref=mine, dst_ref=mine,
            send_sem=max_send.at[i, step], recv_sem=max_recv.at[i, step],
            device_id={"replica": peer(step)}, device_id_type=MESH,
        )

    together = 4
    for i in range(pieces):
        for copy in loads(i):
            copy.wait()

        @pl.loop(0, per_piece // together)
        def _(group):
            for j in range(together):
                block = i * per_piece + group * together + j
                max_slots[me, pl.ds(block, 1), :] = jnp.max(jnp.abs(delta(block)).T, axis=0, keepdims=True)

        if i == 0:
            pl.semaphore_wait(barrier, workers + shards - 2)

        @pl.loop(1, workers)
        def _(step):
            max_copy(i, step).start()

    momentum_copy.start()
    for i in range(pieces):

        @pl.loop(1, workers)
        def _(step):
            max_copy(i, step).wait()

    absmax = max_slots[0]
    for w in range(1, workers):
        absmax = jnp.maximum(absmax, max_slots[w])
    max_out[...] = absmax
    inverse[...] = grid_levels / (absmax + epsilon)
    spread[...] = (absmax + epsilon) / (grid_levels * workers)

    def encode(target, rows_at, put):
        for i in range(blocks_each):
            block = target * blocks_each + i
            values = delta(block, rows_at) * column_of(inverse[pl.ds(block, 1), :][:, rows_at])
            nearest = (values + SHIFT) - SHIFT
            rest = smooth_rest(smooth_rest(values - nearest))
            put(i, (nearest + rest).astype(jnp.bfloat16))

    def far_first(turn):
        return 1 + lax.rem(turn - 1 + (workers // 2 - 1), workers - 1)

    def enc_copy(part, turn):
        step = far_first(turn)
        return pltpu.make_async_remote_copy(
            src_ref=encoded.at[part, peer(step)], dst_ref=arrived.at[part, me],
            send_sem=enc_send.at[part, step], recv_sem=enc_recv.at[part, step],
            device_id={"replica": peer(step)}, device_id_type=MESH,
        )

    for part in range(parts):
        rows_at = slice(part * half, (part + 1) * half)

        @pl.loop(1, workers)
        def _(turn):
            target = peer(far_first(turn))

            def put(i, value):
                encoded[part, target, :, i * BLOCK : (i + 1) * BLOCK] = value

            encode(target, rows_at, put)

            @pl.when(turn > 1)
            def _():
                enc_copy(part, turn - 1).start()

        def put_own(i, value):
            total[rows_at, i * BLOCK : (i + 1) * BLOCK] = value.astype(jnp.float32)

        encode(me, rows_at, put_own)
        enc_copy(part, workers - 1).start()

    pairs = workers // 2
    low = lax.rem(me, 2)
    high = me // 2
    partner = me + 1 - 2 * low

    def place(worker, part):
        return grad_out.at[
            part * half : (part + 1) * half, pl.ds(pl.multiple_of(worker * width, BLOCK), width)
        ]

    def ring_origin(step):
        return lax.rem(high + pairs - step, pairs) * 2 + low

    def gat_copy(part, step):
        return pltpu.make_async_remote_copy(
            src_ref=share.at[part], dst_ref=place(me, part),
            send_sem=gat_send.at[part, step], recv_sem=gat_recv.at[part, step],
            device_id={"replica": lax.rem(high + step, pairs) * 2 + low}, device_id_type=MESH,
        )

    def own_forward(part):
        return pltpu.make_async_remote_copy(
            src_ref=share.at[part], dst_ref=place(me, part),
            send_sem=fwd_send.at[part, 0], recv_sem=fwd_recv.at[part, 0],
            device_id={"replica": partner}, device_id_type=MESH,
        )

    def forward(part, step):
        return pltpu.make_async_remote_copy(
            src_ref=place(ring_origin(step), part), dst_ref=place(ring_origin(step), part),
            send_sem=fwd_send.at[part, step], recv_sem=fwd_recv.at[part, step],
            device_id={"replica": partner}, device_id_type=MESH,
        )

    def own_copy(part):
        return pltpu.make_async_copy(share.at[part], place(me, part), own_sem.at[part])

    def sq_copy(step):
        return pltpu.make_async_remote_copy(
            src_ref=squares.at[me], dst_ref=squares.at[me],
            send_sem=sq_send.at[step], recv_sem=sq_recv.at[step],
            device_id={"replica": peer(step)}, device_id_type=MESH,
        )

    square = jnp.zeros((8, BLOCK), jnp.float32)
    for part in range(parts):
        rows_at = slice(part * half, (part + 1) * half)

        @pl.loop(1, workers)
        def _(turn):
            enc_copy(part, turn).wait()
            total[rows_at, :] += arrived[part, origin(far_first(turn))].astype(jnp.float32)

        for i in range(blocks_each):
            block = me * blocks_each + i
            at = slice(i * BLOCK, (i + 1) * BLOCK)
            value = total[rows_at, at] * column_of(spread[pl.ds(block, 1), :][:, rows_at])
            share[part, :, at] = value.astype(jnp.bfloat16)
            square = square + jnp.sum((value * value).reshape(half // 8, 8, BLOCK), axis=0)

        if part == parts - 1:
            squares[me] = jnp.broadcast_to(jnp.sum(square, axis=0, keepdims=True), (8, BLOCK))

            @pl.loop(1, workers)
            def _(step):
                sq_copy(step).start()

        own_forward(part).start()

        @pl.loop(1, pairs)
        def _(step):
            gat_copy(part, step).start()

        own_copy(part).start()

    for part in range(parts):

        @pl.loop(1, pairs)
        def _(step):
            gat_copy(part, step).wait_recv()
            forward(part, step).start()

    @pl.loop(1, workers)
    def _(step):
        sq_copy(step).wait()

    part_sum = squares[0]
    for w in range(1, workers):
        part_sum = part_sum + squares[w]
    shard_squares[my_shard] = part_sum

    def ss_copy(step):
        return pltpu.make_async_remote_copy(
            src_ref=shard_squares.at[my_shard], dst_ref=shard_squares.at[my_shard],
            send_sem=ss_send.at[step], recv_sem=ss_recv.at[step],
            device_id={"shard": lax.rem(my_shard + step, shards)}, device_id_type=MESH,
        )

    @pl.loop(1, shards)
    def _(step):
        ss_copy(step).start()

    @pl.loop(1, shards)
    def _(step):
        ss_copy(step).wait()

    part_sum = shard_squares[0]
    for s in range(1, shards):
        part_sum = part_sum + shard_squares[s]
    mean = jnp.sum(part_sum, axis=1, keepdims=True) / entry_count
    root_mean = jnp.sqrt(mean + epsilon)
    factor_out[...] = jnp.broadcast_to(jnp.minimum(1.0, clip_level / root_mean), factor_out.shape)

    for part in range(parts):
        own_copy(part).wait()

        @pl.loop(1, pairs)
        def _(step):
            gat_copy(part, step).wait_send()
            forward(part, step).wait()

        own_forward(part).wait()

    momentum_copy.wait()


def exchange(outer_params, local_params, momentum):
    workers = lax.axis_size("replica")
    shards = lax.axis_size("shard")
    rows, cols = outer_params.shape
    blocks = cols // BLOCK
    width = cols // workers
    parts = 2
    half = rows // parts
    dma = pltpu.SemaphoreType.DMA
    vmem = pl.BlockSpec(memory_space=pltpu.VMEM)
    hbm = pl.BlockSpec(memory_space=pltpu.HBM)
    anywhere = pl.BlockSpec(memory_space=pl.ANY)
    return pl.pallas_call(
        functools.partial(exchange_kernel, workers, shards, rows * shards * cols),
        out_shape=(
            jax.ShapeDtypeStruct((rows, cols), jnp.bfloat16),
            jax.ShapeDtypeStruct((rows, cols), jnp.float32),
            jax.ShapeDtypeStruct((blocks, rows), jnp.float32),
            jax.ShapeDtypeStruct((8, BLOCK), jnp.float32),
        ),
        in_specs=[hbm, hbm, hbm],
        out_specs=(anywhere, anywhere, vmem, vmem),
        scratch_shapes=[
            pltpu.VMEM((rows, cols), jnp.float32),
            pltpu.VMEM((rows, cols), jnp.bfloat16),
            pltpu.VMEM((workers, blocks, rows), jnp.float32),
            pltpu.VMEM((blocks, rows), jnp.float32),
            pltpu.VMEM((blocks, rows), jnp.float32),
            pltpu.VMEM((parts, workers, half, width), jnp.bfloat16),
            pltpu.VMEM((parts, workers, half, width), jnp.bfloat16),
            pltpu.VMEM((rows, width), jnp.float32),
            pltpu.VMEM((parts, half, width), jnp.bfloat16),
            pltpu.VMEM((workers, 8, BLOCK), jnp.float32),
            pltpu.VMEM((shards, 8, BLOCK), jnp.float32),
            dma((2, 4)),
            dma((4, workers)), dma((4, workers)),
            dma((parts, workers)), dma((parts, workers)),
            dma((workers,)), dma((workers,)),
            dma((shards,)), dma((shards,)),
            dma((parts, workers // 2)), dma((parts, workers // 2)),
            dma((parts, workers // 2)), dma((parts, workers // 2)),
            dma((parts,)), dma(()),
        ],
        compiler_params=pltpu.CompilerParams(
            collective_id=0, has_side_effects=True, vmem_limit_bytes=16 * 2**20
        ),
        cost_estimate=pl.CostEstimate(
            flops=50 * rows * cols, bytes_accessed=8 * rows * cols * 4, transcendentals=0
        ),
    )(*(pltpu.with_memory_space_constraint(x, pltpu.HBM) for x in (outer_params, local_params, momentum)))


def finish_kernel(
    factor_ref, outer_ref, gradient_ref, momentum_ref, max_ref, params_out, next_out, max_out,
    params_v, next_v, sem, max_sem,
):
    tiles = sem.shape[1]
    rows = outer_ref.shape[0] // tiles
    maxima = pltpu.make_async_copy(max_ref, max_out, max_sem)
    maxima.start()

    def stores(tile):
        at = pl.ds(tile * rows, rows)
        return (
            pltpu.make_async_copy(next_v.at[at], next_out.at[at], sem.at[0, tile]),
            pltpu.make_async_copy(params_v.at[at], params_out.at[at], sem.at[1, tile]),
        )

    factor = factor_ref[0:1, 0:1]

    @pl.loop(0, tiles)
    def _(tile):
        at = pl.ds(pl.multiple_of(tile * rows, rows), rows)
        clipped = factor * gradient_ref[at, :].astype(jnp.float32)
        momentum_next = outer_decay * momentum_ref[at, :] + clipped
        next_v[at, :] = momentum_next
        params_v[at, :] = outer_ref[at, :] - outer_rate * (clipped + outer_decay * momentum_next)
        for copy in stores(tile):
            copy.start()

    @pl.loop(0, tiles)
    def _(tile):
        for copy in stores(tile):
            copy.wait()

    maxima.wait()


def finish(factor, outer_params, gradient, momentum, absmax):
    rows, cols = outer_params.shape
    tiles = rows // 16
    vmem = pl.BlockSpec(memory_space=pltpu.VMEM)
    hbm = pl.BlockSpec(memory_space=pltpu.HBM)
    return pl.pallas_call(
        finish_kernel,
        out_shape=(
            pltpu.HBM((rows, cols), jnp.float32),
            pltpu.HBM((rows, cols), jnp.float32),
            pltpu.HBM(absmax.shape, jnp.float32),
        ),
        in_specs=[vmem] * 5,
        out_specs=(hbm, hbm, hbm),
        scratch_shapes=[
            pltpu.VMEM((rows, cols), jnp.float32),
            pltpu.VMEM((rows, cols), jnp.float32),
            pltpu.SemaphoreType.DMA((2, tiles)),
            pltpu.SemaphoreType.DMA(()),
        ],
        compiler_params=pltpu.CompilerParams(vmem_limit_bytes=16 * 2**20),
        cost_estimate=pl.CostEstimate(
            flops=6 * rows * cols, bytes_accessed=18 * rows * cols, transcendentals=0
        ),
    )(factor, outer_params, gradient, momentum, absmax)


def per_device(outer_params, local_params, momentum):
    gradient, momentum, absmax, factor = exchange(outer_params, local_params, momentum)
    return finish(factor, outer_params, gradient, momentum, absmax)


def solution(mesh):
    return jax.shard_map(
        per_device,
        mesh=mesh,
        in_specs=(P("shard", None), P("replica", "shard", None), P("shard", None)),
        out_specs=(P("shard", None), P("shard", None), P(None, "shard")),
        check_vma=False,
    )
```

profile of v0, /device:TPU:0, one launch (start us, length us, event | category | flops | bytes accessed | tf_op | source)
XLA Modules:
  0.0 55.2 jit_solution(493545278055812867)
XLA Ops:
  0.6 0.0 copy-start
  0.6 52.3 %shard_map.58 = (bf16[128,4096]{1,0:T(8,128)(2,1)S(1)}, f32[128,4096]{1,0:T(8,128)S(1)}, f32[32,128]{1,0:T(8,128)S(1)}, f32[8,128]{1,0:T(8,128)S(1)}) custom-call(f32[128,4096]{1,0:T(8,128)} %outer_ref.1, bf16[1,128,4096]{2,1,0:T(8,128)(2,1)} %local_hbm.1, f32[128,4096]{1,0:T(8,128)} %momentum_hbm.1), custom_call_target="tpu_custom_call" | custom-call | flops 26214400 | bytes 16777216 | tf_op jit(solution)/shard_map/pallas_call | solution.py:306
  53.0 0.0 copy-done
  53.0 2.2 %shard_map.59 = (f32[128,4096]{1,0:T(8,128)}, f32[128,4096]{1,0:T(8,128)}, f32[32,128]{1,0:T(8,128)}) custom-call(f32[8,128]{1,0:T(8,128)S(1)} %get-tuple-element.7.factor_ref, f32[128,4096]{1,0:T(8,128)S(1)} %copy-done, bf16[128,4096]{1,0:T(8,128)(2,1)S(1)} %get-tuple-element.8.gradient_ref, f32[128,4096]{1,0:T(8,128)S(1)} %get-tuple-element.9.momentum_ref, ...), custom_call_target="tpu_custom_call" | custom-call | flops 3145728 | bytes 9437184 | tf_op jit(solution)/shard_map/pallas_call | solution.py:387
Async XLA Ops:
  0.6 52.3 %copy-start = (f32[128,4096]{1,0:T(8,128)S(1)}, f32[128,4096]{1,0:T(8,128)}, u32[]{:S(2)}) copy-start(f32[128,4096]{1,0:T(8,128)} %outer_ref.1) | copy-start | bytes 6291460
where the time goes:
time: 55.4 us; the launch traced here: 55.2 us
  Pallas kernels  54.6 us (99%)
  between operations  0.65 us (1%)
    pallas_call x1, Pallas kernels, exchange(): pl.pallas_call(functools.partial(exchange_kernel, workers, shards, rows *...  52.3 us
    pallas_call x1, Pallas kernels, finish(): pl.pallas_call(finish_kernel, out_shape=(pltpu.HBM((rows, cols), jnp.floa...  2.23 us

commit v1 on v0

v1 whole, which is shorter than its diff:
```python
import functools

import jax
import jax.numpy as jnp
from jax import lax
from jax.experimental import pallas as pl
from jax.experimental.pallas import tpu as pltpu
from jax.sharding import PartitionSpec as P

BLOCK = 128
MESH = pl.DeviceIdType.MESH

epsilon = 1e-06
clip_level = 0.5
outer_rate = 0.7
outer_decay = 0.9
grid_levels = 7.0

SMOOTH = (6.57973588, -12.98785441, 12.20756634, -6.687892761, 2.368806331, -0.5120006377)
SHIFT = 1.5 * 2.0**23
SQUARE = 4
CODE_RANGE = 112.0
PARTS = 4


def smooth_rest(rest):
    square = rest * rest
    value = SMOOTH[-1]
    for coefficient in SMOOTH[-2::-1]:
        value = value * square + coefficient
    return rest * square * value


def column_of(row):
    return jnp.broadcast_to(row, (BLOCK, row.shape[1])).T


def encode(deltas, inverse):
    values = deltas * inverse
    nearest = (values + SHIFT) - SHIFT
    rest = smooth_rest(smooth_rest(values - nearest))
    return (nearest + rest).astype(jnp.bfloat16).astype(jnp.float32)


def pack(total, most):
    return jnp.exp2(total * (CODE_RANGE / most)).astype(jnp.bfloat16)


def unpack(code, most):
    return jnp.log2(code.astype(jnp.float32)) * (most / CODE_RANGE)


def exchange_kernel(
    workers, shards, entry_count,
    outer_hbm, local_hbm, momentum_hbm, gradient_out, momentum_out, max_out, factor_out,
    outer_v, local_v, raw, local_max, max_slots, inverse, spread, own_sum, staged, arrived, gathered, squares, shard_squares,
    load_sem, raw_send, raw_recv, max_send, max_recv, top_send, top_recv, sum_send, sum_recv,
    sq_send, sq_recv, ss_send, ss_recv, gat_send, gat_recv, fwd_send, fwd_recv, momentum_sem,
):
    me = lax.axis_index("replica")
    my_shard = lax.axis_index("shard")
    rows, cols = outer_v.shape
    quarter = cols // SQUARE
    width = cols // workers
    blocks_each = width // BLOCK
    quarter_blocks = quarter // BLOCK
    squares_count = workers // SQUARE
    parts = gathered.shape[0]
    part_rows = rows // parts
    most_square = grid_levels * SQUARE
    most_all = grid_levels * workers

    position = lax.rem(me, SQUARE)
    my_square = me // SQUARE
    low = lax.rem(me, 2)
    high = me // 2
    pairs = workers // 2
    flipped = position + 1 - 2 * low
    across = lax.rem(position + 2, SQUARE)
    diagonal = lax.rem(flipped + 2, SQUARE)
    mates = (diagonal, flipped, across)
    partner = me + 1 - 2 * low

    def peer(step):
        return lax.rem(me + step, workers)

    def span(start, size):
        return pl.ds(pl.multiple_of(start, BLOCK), size)

    def loads(i):
        part = pl.ds(i * quarter, quarter)
        return (
            pltpu.make_async_copy(outer_hbm.at[:, part], outer_v.at[:, part], load_sem.at[0, i]),
            pltpu.make_async_copy(local_hbm.at[0, :, part], local_v.at[:, part], load_sem.at[1, i]),
        )

    for i in range(SQUARE):
        for copy in loads(i):
            copy.start()
    momentum_copy = pltpu.make_async_copy(momentum_hbm, momentum_out, momentum_sem)

    barrier = pltpu.get_barrier_semaphore()

    @pl.loop(1, workers)
    def _(step):
        pl.semaphore_signal(barrier, inc=1, device_id={"replica": peer(step)}, device_id_type=MESH)

    @pl.loop(1, shards)
    def _(step):
        pl.semaphore_signal(
            barrier, inc=1, device_id={"shard": lax.rem(my_shard + step, shards)}, device_id_type=MESH
        )

    def rows_of(part):
        return pl.ds(pl.multiple_of(part * part_rows, part_rows), part_rows)

    def raw_copy(part, mate):
        return pltpu.make_async_remote_copy(
            src_ref=local_v.at[rows_of(part), span(mates[mate] * quarter, quarter)],
            dst_ref=raw.at[mate, rows_of(part), :],
            send_sem=raw_send.at[part, mate], recv_sem=raw_recv.at[part, mate],
            device_id={"replica": my_square * SQUARE + mates[mate]}, device_id_type=MESH,
        )

    def max_copy(step):
        target = lax.rem(peer(step), SQUARE)
        return pltpu.make_async_remote_copy(
            src_ref=local_max.at[pl.ds(pl.multiple_of(target * quarter_blocks, quarter_blocks), quarter_blocks)],
            dst_ref=max_slots.at[me],
            send_sem=max_send.at[step], recv_sem=max_recv.at[step],
            device_id={"replica": peer(step)}, device_id_type=MESH,
        )

    together = min(4, quarter_blocks)
    for i in range(SQUARE):
        for copy in loads(i):
            copy.wait()

        @pl.loop(0, quarter_blocks // together)
        def _(group):
            for j in range(together):
                block = i * quarter_blocks + group * together + j
                at = span(block * BLOCK, BLOCK)
                deltas = outer_v[:, at] - local_v[:, at].astype(jnp.float32)
                local_max[pl.ds(block, 1), :] = jnp.max(jnp.abs(deltas).T, axis=0, keepdims=True)

    mine = pl.ds(pl.multiple_of(position * quarter_blocks, quarter_blocks), quarter_blocks)
    max_slots[me] = local_max[mine]
    pl.semaphore_wait(barrier, workers + shards - 2)

    @pl.loop(1, workers)
    def _(step):
        max_copy(step).start()

    @pl.loop(0, parts)
    def _(part):
        for mate in range(3):
            raw_copy(part, mate).start()

    momentum_copy.start()

    @pl.loop(1, workers)
    def _(step):
        max_copy(step).wait()

    absmax = max_slots[0]
    for w in range(1, workers):
        absmax = jnp.maximum(absmax, max_slots[w])
    max_out[mine] = absmax
    scale = absmax + epsilon

    def top_copy(mate):
        return pltpu.make_async_remote_copy(
            src_ref=max_out.at[mine], dst_ref=max_out.at[mine],
            send_sem=top_send.at[mate], recv_sem=top_recv.at[mate],
            device_id={"replica": my_square * SQUARE + mates[mate]}, device_id_type=MESH,
        )

    quotient = grid_levels / scale
    for block in range(quarter_blocks):
        inverse[:, block * BLOCK : (block + 1) * BLOCK] = column_of(quotient[block : block + 1, :])
    for mate in range(3):
        top_copy(mate).start()

    def spread_column(block):
        row = (max_out[pl.ds(block, 1), :] + epsilon) * (1.0 / (grid_levels * workers))
        spread[:, span(block * BLOCK, BLOCK)] = column_of(row)

    def place(worker):
        return lax.rem(worker, SQUARE) * quarter + (worker // SQUARE) * width

    @pl.loop(0, quarter_blocks)
    def _(block):
        spread_column(position * quarter_blocks + block)

    def square_of(turn):
        return lax.rem(my_square + turn, squares_count)

    def sum_copy(part, turn):
        return pltpu.make_async_remote_copy(
            src_ref=staged.at[square_of(turn), rows_of(part)], dst_ref=arrived.at[my_square, rows_of(part)],
            send_sem=sum_send.at[part, turn], recv_sem=sum_recv.at[part, turn],
            device_id={"replica": square_of(turn) * SQUARE + position}, device_id_type=MESH,
        )

    def square_sum(part, block):
        at_rows = rows_of(part)
        at = span(position * quarter + block * BLOCK, BLOCK)
        here = span(block * BLOCK, BLOCK)
        outer = outer_v[at_rows, at]
        inv = inverse[at_rows, here]
        total = encode(outer - local_v[at_rows, at].astype(jnp.float32), inv)
        for mate in range(3):
            total = total + encode(outer - raw[mate, at_rows, here].astype(jnp.float32), inv)
        return total

    def encode_part(part):
        for mate in range(3):
            raw_copy(part, mate).wait_recv()

        @pl.loop(1, squares_count)
        def _(turn):
            target = square_of(turn)
            for i in range(blocks_each):
                staged[target, rows_of(part), i * BLOCK : (i + 1) * BLOCK] = pack(
                    square_sum(part, target * blocks_each + i), most_square
                )

        for i in range(blocks_each):
            own_sum[rows_of(part), i * BLOCK : (i + 1) * BLOCK] = square_sum(part, my_square * blocks_each + i)

        @pl.loop(1, squares_count)
        def _(turn):
            sum_copy(part, turn).start()

    def gat_copy(part, step):
        return pltpu.make_async_remote_copy(
            src_ref=gathered.at[part, me], dst_ref=gathered.at[part, me],
            send_sem=gat_send.at[part, step], recv_sem=gat_recv.at[part, step],
            device_id={"replica": lax.rem(high + step, pairs) * 2 + low}, device_id_type=MESH,
        )

    def forward(part, step):
        origin = lax.rem(high + pairs - step, pairs) * 2 + low
        return pltpu.make_async_remote_copy(
            src_ref=gathered.at[part, origin], dst_ref=gathered.at[part, origin],
            send_sem=fwd_send.at[part, step], recv_sem=fwd_recv.at[part, step],
            device_id={"replica": partner}, device_id_type=MESH,
        )

    squares[me] = jnp.zeros((8, BLOCK), jnp.float32)

    def finish_part(part):
        @pl.loop(1, squares_count)
        def _(turn):
            sum_copy(part, turn).wait_recv()

        at_rows = rows_of(part)
        square = squares[me]
        for i in range(blocks_each):
            at = slice(i * BLOCK, (i + 1) * BLOCK)

            def add(turn, total):
                origin = lax.rem(my_square + squares_count - turn, squares_count)
                return total + unpack(arrived[origin, at_rows, at], most_square)

            total = lax.fori_loop(1, squares_count, add, own_sum[at_rows, at])
            gathered[part, me, :, at] = pack(total, most_all)
            value = total * spread[at_rows, span(place(me) + i * BLOCK, BLOCK)]
            square = square + jnp.sum((value * value).reshape(part_rows // 8, 8, BLOCK), axis=0)
        squares[me] = square

    def gather_part(part):
        forward(part, 0).start()

        @pl.loop(1, pairs)
        def _(step):
            gat_copy(part, step).start()

    def forward_part(part):
        @pl.loop(1, pairs)
        def _(step):
            gat_copy(part, step).wait_recv()
            forward(part, step).start()

    def sq_copy(step):
        return pltpu.make_async_remote_copy(
            src_ref=squares.at[me], dst_ref=squares.at[me],
            send_sem=sq_send.at[step], recv_sem=sq_recv.at[step],
            device_id={"replica": peer(step)}, device_id_type=MESH,
        )

    def ss_copy(step):
        return pltpu.make_async_remote_copy(
            src_ref=shard_squares.at[my_shard], dst_ref=shard_squares.at[my_shard],
            send_sem=ss_send.at[step], recv_sem=ss_recv.at[step],
            device_id={"shard": lax.rem(my_shard + step, shards)}, device_id_type=MESH,
        )

    for part in range(parts + 1):
        if part < parts:
            encode_part(part)
        if part >= 1:
            finish_part(part - 1)
            if part == parts:
                squares[me] = jnp.broadcast_to(jnp.sum(squares[me], axis=0, keepdims=True), (8, BLOCK))

                @pl.loop(1, workers)
                def _(step):
                    sq_copy(step).start()

            gather_part(part - 1)
        if part >= 2:
            forward_part(part - 2)

    for mate in range(3):
        top_copy(mate).wait()

    @pl.loop(0, SQUARE * quarter_blocks)
    def _(block):
        spread_column(block)

    def decode(part, worker):
        at = span(place(worker), width)
        gradient_out[rows_of(part), at] = unpack(gathered[part, worker], most_all) * spread[rows_of(part), at]

    for part in range(parts):
        @pl.loop(0, pairs)
        def _(step):
            origin = lax.rem(high + pairs - step, pairs) * 2 + low
            if part < parts - 1:
                decode(part, origin)

    forward_part(parts - 1)

    @pl.loop(1, workers)
    def _(step):
        sq_copy(step).wait()

    part_sum = squares[0]
    for w in range(1, workers):
        part_sum = part_sum + squares[w]
    shard_squares[my_shard] = part_sum

    @pl.loop(1, shards)
    def _(step):
        ss_copy(step).start()

    @pl.loop(0, pairs)
    def _(step):
        decode(parts - 1, lax.rem(high + pairs - step, pairs) * 2 + low)

    for part in range(parts):
        @pl.loop(0, pairs)
        def _(step):
            forward(part, step).wait_recv()
            decode(part, lax.rem(high + pairs - step, pairs) * 2 + 1 - low)

    @pl.loop(1, shards)
    def _(step):
        ss_copy(step).wait()

    part_sum = shard_squares[0]
    for s in range(1, shards):
        part_sum = part_sum + shard_squares[s]
    mean = jnp.sum(part_sum, axis=1, keepdims=True) / entry_count
    root_mean = jnp.sqrt(mean + epsilon)
    factor_out[...] = jnp.broadcast_to(jnp.minimum(1.0, clip_level / root_mean), factor_out.shape)

    @pl.loop(0, parts)
    def _(part):
        for mate in range(3):
            raw_copy(part, mate).wait_send()

        @pl.loop(1, squares_count)
        def _(turn):
            sum_copy(part, turn).wait_send()

        @pl.loop(1, pairs)
        def _(step):
            gat_copy(part, step).wait_send()

        @pl.loop(0, pairs)
        def _(step):
            forward(part, step).wait_send()

    momentum_copy.wait()


def exchange(outer_params, local_params, momentum):
    workers = lax.axis_size("replica")
    shards = lax.axis_size("shard")
    rows, cols = outer_params.shape
    blocks = cols // BLOCK
    width = cols // workers
    quarter = cols // SQUARE
    squares_count = workers // SQUARE
    pairs = workers // 2
    parts = PARTS
    dma = pltpu.SemaphoreType.DMA
    vmem = pl.BlockSpec(memory_space=pltpu.VMEM)
    hbm = pl.BlockSpec(memory_space=pltpu.HBM)
    anywhere = pl.BlockSpec(memory_space=pl.ANY)
    return pl.pallas_call(
        functools.partial(exchange_kernel, workers, shards, rows * shards * cols),
        out_shape=(
            jax.ShapeDtypeStruct((rows, cols), jnp.float32),
            jax.ShapeDtypeStruct((rows, cols), jnp.float32),
            jax.ShapeDtypeStruct((blocks, rows), jnp.float32),
            jax.ShapeDtypeStruct((8, BLOCK), jnp.float32),
        ),
        in_specs=[hbm, hbm, hbm],
        out_specs=(vmem, anywhere, vmem, vmem),
        scratch_shapes=[
            pltpu.VMEM((rows, cols), jnp.float32),
            pltpu.VMEM((rows, cols), jnp.bfloat16),
            pltpu.VMEM((3, rows, quarter), jnp.bfloat16),
            pltpu.VMEM((blocks, rows), jnp.float32),
            pltpu.VMEM((workers, blocks // SQUARE, rows), jnp.float32),
            pltpu.VMEM((rows, quarter), jnp.float32),
            pltpu.VMEM((rows, cols), jnp.float32),
            pltpu.VMEM((rows, width), jnp.float32),
            pltpu.VMEM((squares_count, rows, width), jnp.bfloat16),
            pltpu.VMEM((squares_count, rows, width), jnp.bfloat16),
            pltpu.VMEM((parts, workers, rows // parts, width), jnp.bfloat16),
            pltpu.VMEM((workers, 8, BLOCK), jnp.float32),
            pltpu.VMEM((shards, 8, BLOCK), jnp.float32),
            dma((2, SQUARE)),
            dma((parts, 3)), dma((parts, 3)),
            dma((workers,)), dma((workers,)),
            dma((3,)), dma((3,)),
            dma((parts, squares_count)), dma((parts, squares_count)),
            dma((workers,)), dma((workers,)),
            dma((shards,)), dma((shards,)),
            dma((parts, pairs)), dma((parts, pairs)),
            dma((parts, pairs)), dma((parts, pairs)),
            dma(()),
        ],
        compiler_params=pltpu.CompilerParams(
            collective_id=0, has_side_effects=True, vmem_limit_bytes=24 * 2**20
        ),
        cost_estimate=pl.CostEstimate(
            flops=50 * rows * cols, bytes_accessed=8 * rows * cols * 4, transcendentals=0
        ),
    )(*(pltpu.with_memory_space_constraint(x, pltpu.HBM) for x in (outer_params, local_params, momentum)))


def finish_kernel(
    factor_ref, outer_ref, gradient_ref, momentum_ref, max_ref, params_out, next_out, max_out,
    params_v, next_v, sem, max_sem,
):
    tiles = sem.shape[1]
    rows = outer_ref.shape[0] // tiles
    maxima = pltpu.make_async_copy(max_ref, max_out, max_sem)
    maxima.start()

    def stores(tile):
        at = pl.ds(tile * rows, rows)
        return (
            pltpu.make_async_copy(next_v.at[at], next_out.at[at], sem.at[0, tile]),
            pltpu.make_async_copy(params_v.at[at], params_out.at[at], sem.at[1, tile]),
        )

    factor = factor_ref[0:1, 0:1]

    @pl.loop(0, tiles)
    def _(tile):
        at = pl.ds(pl.multiple_of(tile * rows, rows), rows)
        clipped = factor * gradient_ref[at, :]
        momentum_next = outer_decay * momentum_ref[at, :] + clipped
        next_v[at, :] = momentum_next
        params_v[at, :] = outer_ref[at, :] - outer_rate * (clipped + outer_decay * momentum_next)
        for copy in stores(tile):
            copy.start()

    @pl.loop(0, tiles)
    def _(tile):
        for copy in stores(tile):
            copy.wait()

    maxima.wait()


def finish(factor, outer_params, gradient, momentum, absmax):
    rows, cols = outer_params.shape
    tiles = rows // 16
    vmem = pl.BlockSpec(memory_space=pltpu.VMEM)
    hbm = pl.BlockSpec(memory_space=pltpu.HBM)
    return pl.pallas_call(
        finish_kernel,
        out_shape=(
            pltpu.HBM((rows, cols), jnp.float32),
            pltpu.HBM((rows, cols), jnp.float32),
            pltpu.HBM(absmax.shape, jnp.float32),
        ),
        in_specs=[vmem] * 5,
        out_specs=(hbm, hbm, hbm),
        scratch_shapes=[
            pltpu.VMEM((rows, cols), jnp.float32),
            pltpu.VMEM((rows, cols), jnp.float32),
            pltpu.SemaphoreType.DMA((2, tiles)),
            pltpu.SemaphoreType.DMA(()),
        ],
        compiler_params=pltpu.CompilerParams(vmem_limit_bytes=16 * 2**20),
        cost_estimate=pl.CostEstimate(
            flops=6 * rows * cols, bytes_accessed=18 * rows * cols, transcendentals=0
        ),
    )(factor, outer_params, gradient, momentum, absmax)


def per_device(outer_params, local_params, momentum):
    gradient, momentum, absmax, factor = exchange(outer_params, local_params, momentum)
    return finish(factor, outer_params, gradient, momentum, absmax)


def solution(mesh):
    return jax.shard_map(
        per_device,
        mesh=mesh,
        in_specs=(P("shard", None), P("replica", "shard", None), P("shard", None)),
        out_specs=(P("shard", None), P("shard", None), P(None, "shard")),
        check_vma=False,
    )
```

time: 55.4 us -> 45.8 us (0.83)
  Pallas kernels: 54.6 us -> 45 us
    pallas_call x1, Pallas kernels: 52.3 us -> 42.8 us  [exchange(): pl.pallas_call(functools.partial(exchange_kernel, workers, shards, rows *...]
where the time goes in v1:
time: 45.8 us; the launch traced here: 45.7 us
  Pallas kernels  45 us (98%)
  between operations  0.65 us (1%)
    pallas_call x1, Pallas kernels, exchange(): pl.pallas_call(functools.partial(exchange_kernel, workers, shards, rows *...  42.8 us
    pallas_call x1, Pallas kernels, finish(): pl.pallas_call(finish_kernel, out_shape=(pltpu.HBM((rows, cols), jnp.floa...  2.23 us

profile of v1, /device:TPU:0, one launch (start us, length us, event | category | flops | bytes accessed | tf_op | source)
XLA Modules:
  0.0 45.7 jit_solution(6993753570978314274)
XLA Ops:
  0.6 0.0 copy-start
  0.6 42.8 %shard_map.58 = (f32[128,4096]{1,0:T(8,128)S(1)}, f32[128,4096]{1,0:T(8,128)S(1)}, f32[32,128]{1,0:T(8,128)S(1)}, f32[8,128]{1,0:T(8,128)S(1)}) custom-call(f32[128,4096]{1,0:T(8,128)} %outer_ref.1, bf16[1,128,4096]{2,1,0:T(8,128)(2,1)} %local_hbm.1, f32[128,4096]{1,0:T(8,128)} %momentum_hbm.1), custom_call_target="tpu_custom_call" | custom-call | flops 26214400 | bytes 16777216 | tf_op jit(solution)/shard_map/pallas_call | solution.py:404
  43.4 0.0 copy-done
  43.4 2.2 %shard_map.59 = (f32[128,4096]{1,0:T(8,128)}, f32[128,4096]{1,0:T(8,128)}, f32[32,128]{1,0:T(8,128)}) custom-call(f32[8,128]{1,0:T(8,128)S(1)} %get-tuple-element.7.factor_ref, f32[128,4096]{1,0:T(8,128)S(1)} %copy-done, f32[128,4096]{1,0:T(8,128)S(1)} %get-tuple-element.8.gradient_ref, f32[128,4096]{1,0:T(8,128)S(1)} %get-tuple-element.9.momentum_ref, ...), custom_call_target="tpu_custom_call" | custom-call | flops 3145728 | bytes 9437184 | tf_op jit(solution)/shard_map/pallas_call | solution.py:489
Async XLA Ops:
  0.6 42.8 %copy-start = (f32[128,4096]{1,0:T(8,128)S(1)}, f32[128,4096]{1,0:T(8,128)}, u32[]{:S(2)}) copy-start(f32[128,4096]{1,0:T(8,128)} %outer_ref.1) | copy-start | bytes 6291460

commit v2 on v0

v2 whole, which is shorter than its diff:
```python
import functools

import jax
import jax.numpy as jnp
from jax import lax
from jax.experimental import pallas as pl
from jax.experimental.pallas import tpu as pltpu
from jax.sharding import PartitionSpec as P

BLOCK = 128
MESH = pl.DeviceIdType.MESH

epsilon = 1e-06
clip_level = 0.5
outer_rate = 0.7
outer_decay = 0.9
grid_levels = 7.0

SMOOTH = (6.57973588, -12.98785441, 12.20756634, -6.687892761, 2.368806331, -0.5120006377)
SHIFT = 1.5 * 2.0**23
SQUARE = 4
CODE_RANGE = 112.0
SPLIT = (1, 2, 2, 2, 1)
DIRECT = 1
PIECES = 8
AHEAD = 3
TURN = {"encode": 0.0, "quad": 2.2, "finish": 5.75, "pass": 6.8, "sent": 7.0, "decode": 7.1}
FILL = (1.6, 5.3, 5.35)


def smooth_rest(rest):
    square = rest * rest
    value = SMOOTH[-1]
    for coefficient in SMOOTH[-2::-1]:
        value = value * square + coefficient
    return rest * square * value


def column_of(row):
    return jnp.broadcast_to(row, (BLOCK, row.shape[1])).T


def encode(deltas, inverse):
    values = deltas * inverse
    nearest = (values + SHIFT) - SHIFT
    rest = smooth_rest(smooth_rest(values - nearest))
    return (nearest + rest).astype(jnp.bfloat16).astype(jnp.float32)


def pack(total, most):
    return jnp.exp2(total * (CODE_RANGE / most)).astype(jnp.bfloat16)


def unpack(code, most):
    return jnp.log2(code.astype(jnp.float32)) * (most / CODE_RANGE)


def exchange_kernel(
    workers, shards, entry_count,
    outer_hbm, local_hbm, momentum_hbm, outer_v, gradient_out, momentum_out, max_out, factor_out,
    local_v, raw, local_max, max_slots, inverse, spread, pair_own, pair_out, pair_in, quads,
    gathered, squares,
    load_sem, raw_send, raw_recv, max_send, max_recv, top_send, top_recv, pair_send, pair_recv,
    quad_send, quad_recv, line_send, line_recv, pass_send, pass_recv, sq_send, sq_recv, momentum_sem,
):
    me = lax.axis_index("replica")
    my_shard = lax.axis_index("shard")
    rows, cols = outer_v.shape
    quarter, eighth = cols // 4, cols // 8
    group_blocks = quarter // BLOCK
    half_blocks = eighth // BLOCK
    count = workers // SQUARE
    parts = len(SPLIT)
    starts = [rows * sum(SPLIT[:part]) // sum(SPLIT) for part in range(parts + 1)]
    most = [grid_levels * 2, grid_levels * SQUARE, grid_levels * workers]

    position = lax.rem(me, SQUARE)
    my_square = me // SQUARE
    low = lax.rem(position, 2)
    beside = position + 1 - 2 * low
    across = lax.rem(position + 2, SQUARE)
    diagonal = lax.rem(beside + 2, SQUARE)
    mates = (diagonal, beside, across)

    def pick(kind, first, second):
        return (first, second)[kind]

    def in_square(place):
        return {"replica": my_square * SQUARE + place}

    def first_mate(kind):
        return in_square(pick(kind, beside, across))

    def second_mate(kind):
        return in_square(pick(kind, across, beside))

    def group_of(kind, place):
        return kind * 2 + pick(kind, lax.rem(place, 2), place // 2)

    def half_of(kind, place):
        return pick(kind, place // 2, lax.rem(place, 2))

    def span(start, size):
        return pl.ds(pl.multiple_of(start, BLOCK), size)

    def rows_of(part):
        return slice(starts[part], starts[part + 1])

    def group_rows(group):
        return pl.ds(pl.multiple_of(group * group_blocks, group_blocks), group_blocks)

    def place_of(kind, place):
        return group_of(kind, place) * quarter + half_of(kind, place) * eighth

    def square_at(step):
        return lax.rem(my_square + step, count)

    def square_from(step):
        return lax.rem(my_square + count - step, count)

    def peer(step):
        return lax.rem(me + step, workers)

    def in_line(step):
        return {"replica": square_at(step) * SQUARE + position}

    def in_shard(step):
        return {"shard": lax.rem(my_shard + step, shards)}

    pieces = load_sem.shape[1]
    piece = cols // pieces

    def loads(i):
        part = pl.ds(i * piece, piece)
        return (
            pltpu.make_async_copy(outer_hbm.at[:, part], outer_v.at[:, part], load_sem.at[0, i]),
            pltpu.make_async_copy(local_hbm.at[0, :, part], local_v.at[:, part], load_sem.at[1, i]),
        )

    for i in range(pieces):
        for copy in loads(i):
            copy.start()

    barrier = pltpu.get_barrier_semaphore()
    for step in range(1, workers):
        pl.semaphore_signal(barrier, inc=1, device_id={"replica": peer(step)}, device_id_type=MESH)
    beyond = [in_shard(step) for step in range(1, shards)]
    beyond += [in_square(mate) | in_shard(step) for mate in mates for step in range(1, shards)]
    for device in beyond:
        pl.semaphore_signal(barrier, inc=1, device_id=device, device_id_type=MESH)

    def remote(source, target, send, recv, device):
        return pltpu.make_async_remote_copy(
            src_ref=source, dst_ref=target, send_sem=send, recv_sem=recv, device_id=device, device_id_type=MESH
        )

    def wait_bytes(ref, sem):
        pltpu.make_async_copy(ref, ref, sem).wait()

    def raw_copy(kind, part):
        other = (kind * 4 + 1 - group_of(kind, position)) * quarter
        return remote(
            local_v.at[rows_of(part), span(other, quarter)], raw.at[kind, rows_of(part)],
            raw_send, raw_recv.at[kind, part], first_mate(kind),
        )

    per_piece = piece // BLOCK
    for i in range(pieces):
        for copy in loads(i):
            copy.wait()

        for j in range(per_piece):
            block = i * per_piece + j
            at = slice(block * BLOCK, (block + 1) * BLOCK)
            deltas = outer_v[:, at] - local_v[:, at].astype(jnp.float32)
            local_max[block : block + 1, :] = jnp.max(jnp.abs(deltas).T, axis=0, keepdims=True)

    pl.semaphore_wait(barrier, workers - 1 + len(beyond))

    for step in range(workers - 1, 0, -1):
        for kind in range(2):
            remote(
                local_max.at[group_rows(group_of(kind, lax.rem(peer(step), SQUARE)))], max_slots.at[step, kind],
                max_send, max_recv, {"replica": peer(step)},
            ).start()

    def raw_start(part):
        for kind in range(2):
            raw_copy(kind, part).start()

    ahead = min(AHEAD, parts)
    for part in range(ahead):
        raw_start(part)

    momentum_copy = pltpu.make_async_copy(momentum_hbm, momentum_out, momentum_sem)
    momentum_copy.start()
    arrived = max_slots.at[pl.ds(1, workers - 1)]
    wait_bytes(arrived, max_recv)

    def top_copy(kind):
        at = group_rows(group_of(kind, position))
        return remote(max_out.at[at], max_out.at[at], top_send, top_recv, first_mate(kind))

    def invert(kind):
        absmax = local_max[group_rows(group_of(kind, position))]
        for step in range(1, workers):
            absmax = jnp.maximum(absmax, max_slots[step, kind])
        max_out[group_rows(group_of(kind, position))] = absmax
        quotient = grid_levels / (absmax + epsilon)
        for block in range(group_blocks):
            inverse[kind, :, block * BLOCK : (block + 1) * BLOCK] = column_of(quotient[block : block + 1, :])

    def top_start():
        for kind in range(2):
            top_copy(kind).start()

    def top_wait():
        wait_bytes(max_slots.at[0], top_recv)

    def spread_group(group):
        share = (max_out[group_rows(group)] + epsilon) * (1.0 / (grid_levels * workers))
        for block in range(group_blocks):
            spread[:, span(group * quarter + block * BLOCK, BLOCK)] = column_of(share[block : block + 1, :])

    def own_spread():
        for kind in range(2):
            spread_group(group_of(kind, position))

    def other_spread(kind):
        spread_group(kind * 4 + 1 - group_of(kind, position))

    def pair_sum(kind, part, block):
        at_rows = rows_of(part)
        at = span(group_of(kind, position) * quarter + block * BLOCK, BLOCK)
        here = span(block * BLOCK, BLOCK)
        outer = outer_v[at_rows, at]
        inv = inverse[kind, at_rows, here]
        return encode(outer - local_v[at_rows, at].astype(jnp.float32), inv) + encode(
            outer - raw[kind, at_rows, here].astype(jnp.float32), inv
        )

    def pair_copy(kind, part):
        return remote(
            pair_out.at[kind, rows_of(part)], pair_in.at[kind, rows_of(part)],
            pair_send, pair_recv.at[kind, part], second_mate(kind),
        )

    def encode_part(kind, part):
        raw_copy(kind, part).wait_recv()
        mine = half_of(kind, position)
        for i in range(half_blocks):
            pair_out[kind, rows_of(part), i * BLOCK : (i + 1) * BLOCK] = pack(
                pair_sum(kind, part, (1 - mine) * half_blocks + i), most[0]
            )
        for i in range(half_blocks):
            pair_own[kind, rows_of(part), i * BLOCK : (i + 1) * BLOCK] = pair_sum(
                kind, part, mine * half_blocks + i
            )
        pair_copy(kind, part).start()

    def quad_part(kind, part):
        pair_copy(kind, part).wait_recv()
        at = (kind, rows_of(part))
        quads[my_square, kind, rows_of(part)] = pack(pair_own[at] + unpack(pair_in[at], most[0]), most[1])
        for step in range(1, count):
            slot = quads.at[my_square, kind, rows_of(part)]
            remote(slot, slot, quad_send, quad_recv.at[part, step], in_line(step)).start()

    def line_copy(part):
        slot = gathered.at[position, :, rows_of(part)]
        return remote(slot, slot, line_send, line_recv.at[part], in_square(across))

    def direct(part):
        return part >= parts - DIRECT

    def pass_copy(part, side):
        alone = side == 1 and direct(part)
        slot = gathered.at[across if side == 1 and not alone else position, :, rows_of(part)]
        return remote(slot, slot, pass_send, pass_recv.at[part, side], in_square(diagonal if alone else beside))

    mine = my_shard * SQUARE + position
    squares[mine] = jnp.zeros((8, BLOCK), jnp.float32)

    def finish_part(part):
        for step in range(1, count):
            wait_bytes(quads.at[square_from(step), :, rows_of(part)], quad_recv.at[part, step])

        at_rows = rows_of(part)
        square = squares[mine]
        for kind in range(2):
            for i in range(half_blocks):
                at = slice(i * BLOCK, (i + 1) * BLOCK)
                total = unpack(quads[0, kind, at_rows, at], most[1])
                for other in range(1, count):
                    total = total + unpack(quads[other, kind, at_rows, at], most[1])
                gathered[position, kind, at_rows, at] = pack(total, most[2])
                value = total * spread[at_rows, span(place_of(kind, position) + i * BLOCK, BLOCK)]
                square = square + jnp.sum((value * value).reshape(-1, 8, BLOCK), axis=0)
        squares[mine] = square

    def gather_part(part):
        if direct(part):
            pass_copy(part, 1).start()
        line_copy(part).start()
        pass_copy(part, 0).start()

    def pass_part(part):
        line_copy(part).wait_recv()
        if not direct(part):
            pass_copy(part, 1).start()

    def decode(part, place):
        for kind in range(2):
            at = span(place_of(kind, place), eighth)
            gradient_out[rows_of(part), at] = unpack(gathered[place, kind, rows_of(part)], most[2]) * spread[rows_of(part), at]

    def decode_line(part):
        decode(part, position)
        decode(part, across)

    def decode_part(part):
        pass_copy(part, 0).wait_recv()
        decode(part, beside)
        pass_copy(part, 1).wait_recv()
        decode(part, diagonal)

    def squares_start():
        squares[mine] = jnp.broadcast_to(jnp.sum(squares[mine], axis=0, keepdims=True), (8, BLOCK))
        for device in [in_square(mate) for mate in mates] + beyond[::-1]:
            remote(squares.at[mine], squares.at[mine], sq_send, sq_recv, device).start()

    def sent_all():
        wait_bytes(raw, raw_send)
        wait_bytes(arrived, max_send)
        wait_bytes(max_slots.at[0], top_send)
        wait_bytes(pair_out, pair_send)
        wait_bytes(quads.at[pl.ds(0, count - 1)], quad_send)
        momentum_copy.wait()

    stages = []
    last = parts - 1
    for part in range(parts):
        for kind in range(2):
            stages.append((part + TURN["encode"] + 0.5 * kind, encode_part, (kind, part)))
            stages.append((part + TURN["quad"] + 0.5 * kind, quad_part, (kind, part)))
        if part + ahead < parts:
            stages.append((part + TURN["encode"] + 0.55, raw_start, (part + ahead,)))
        stages.append((part + TURN["finish"], finish_part, (part,)))
        if part == last:
            stages.append((part + TURN["finish"], squares_start, ()))
        stages.append((part + TURN["finish"], gather_part, (part,)))
        stages.append((part + TURN["pass"], pass_part, (part,)))
        stages.append((part * 0.01 + last + TURN["decode"], decode_line, (part,)))
        stages.append((part * 0.01 + last + TURN["decode"] + 0.05, decode_part, (part,)))
    for kind in range(2):
        stages.append((kind * 0.5 - 0.1, invert, (kind,)))
        stages.append((FILL[1 + kind], other_spread, (kind,)))
    stages.append((0.9, top_start, ()))
    stages.append((FILL[1] - 0.01, top_wait, ()))
    stages.append((FILL[0], own_spread, ()))
    stages.append((last + TURN["sent"], sent_all, ()))
    for _, stage, given in sorted(stages, key=lambda stage: stage[0]):
        stage(*given)

    others = squares.at[pl.ds(0, SQUARE * shards - 1)]
    wait_bytes(others, sq_recv)
    part_sum = squares[0]
    for slot in range(1, SQUARE * shards):
        part_sum = part_sum + squares[slot]
    mean = jnp.sum(part_sum, axis=1, keepdims=True) / entry_count
    root_mean = jnp.sqrt(mean + epsilon)
    factor_out[...] = jnp.broadcast_to(jnp.minimum(1.0, clip_level / root_mean), factor_out.shape)
    wait_bytes(others, sq_send)
    wait_bytes(gathered.at[0], line_send)
    wait_bytes(gathered.at[pl.ds(0, 2)], pass_send)


def exchange(outer_params, local_params, momentum):
    workers = lax.axis_size("replica")
    shards = lax.axis_size("shard")
    rows, cols = outer_params.shape
    blocks = cols // BLOCK
    quarter, eighth = cols // 4, cols // 8
    count = workers // SQUARE
    parts = len(SPLIT)
    dma = pltpu.SemaphoreType.DMA
    vmem = pl.BlockSpec(memory_space=pltpu.VMEM)
    hbm = pl.BlockSpec(memory_space=pltpu.HBM)
    anywhere = pl.BlockSpec(memory_space=pl.ANY)
    return pl.pallas_call(
        functools.partial(exchange_kernel, workers, shards, rows * shards * cols),
        out_shape=(
            jax.ShapeDtypeStruct((rows, cols), jnp.float32),
            jax.ShapeDtypeStruct((rows, cols), jnp.float32),
            jax.ShapeDtypeStruct((rows, cols), jnp.float32),
            jax.ShapeDtypeStruct((blocks, rows), jnp.float32),
            jax.ShapeDtypeStruct((8, BLOCK), jnp.float32),
        ),
        in_specs=[hbm, hbm, hbm],
        out_specs=(vmem, vmem, anywhere, vmem, vmem),
        scratch_shapes=[
            pltpu.VMEM((rows, cols), jnp.bfloat16),
            pltpu.VMEM((2, rows, quarter), jnp.bfloat16),
            pltpu.VMEM((blocks, rows), jnp.float32),
            pltpu.VMEM((workers, 2, blocks // 4, rows), jnp.float32),
            pltpu.VMEM((2, rows, quarter), jnp.float32),
            pltpu.VMEM((rows, cols), jnp.float32),
            pltpu.VMEM((2, rows, eighth), jnp.float32),
            pltpu.VMEM((2, rows, eighth), jnp.bfloat16),
            pltpu.VMEM((2, rows, eighth), jnp.bfloat16),
            pltpu.VMEM((count, 2, rows, eighth), jnp.bfloat16),
            pltpu.VMEM((SQUARE, 2, rows, eighth), jnp.bfloat16),
            pltpu.VMEM((SQUARE * shards, 8, BLOCK), jnp.float32),
            dma((2, PIECES)),
            dma(()), dma((2, parts)),
            dma(()), dma(()),
            dma(()), dma(()),
            dma(()), dma((2, parts)),
            dma(()), dma((parts, count)),
            dma(()), dma((parts,)),
            dma(()), dma((parts, 2)),
            dma(()), dma(()),
            dma(()),
        ],
        compiler_params=pltpu.CompilerParams(
            collective_id=0, has_side_effects=True, vmem_limit_bytes=24 * 2**20
        ),
        cost_estimate=pl.CostEstimate(
            flops=50 * rows * cols, bytes_accessed=8 * rows * cols * 4, transcendentals=0
        ),
    )(*(pltpu.with_memory_space_constraint(x, pltpu.HBM) for x in (outer_params, local_params, momentum)))


def finish_kernel(
    factor_ref, outer_ref, gradient_ref, momentum_ref, max_ref, params_out, next_out, max_out,
    params_v, next_v, sem, max_sem,
):
    tiles = sem.shape[1]
    rows = outer_ref.shape[0] // tiles
    maxima = pltpu.make_async_copy(max_ref, max_out, max_sem)
    maxima.start()

    def stores(tile):
        at = pl.ds(tile * rows, rows)
        return (
            pltpu.make_async_copy(next_v.at[at], next_out.at[at], sem.at[0, tile]),
            pltpu.make_async_copy(params_v.at[at], params_out.at[at], sem.at[1, tile]),
        )

    factor = factor_ref[0:1, 0:1]

    @pl.loop(0, tiles)
    def _(tile):
        at = pl.ds(pl.multiple_of(tile * rows, rows), rows)
        clipped = factor * gradient_ref[at, :]
        momentum_next = outer_decay * momentum_ref[at, :] + clipped
        next_v[at, :] = momentum_next
        params_v[at, :] = outer_ref[at, :] - outer_rate * (clipped + outer_decay * momentum_next)
        for copy in stores(tile):
            copy.start()

    @pl.loop(0, tiles)
    def _(tile):
        for copy in stores(tile):
            copy.wait()

    maxima.wait()


def finish(factor, outer_params, gradient, momentum, absmax):
    rows, cols = outer_params.shape
    tiles = rows // 16
    vmem = pl.BlockSpec(memory_space=pltpu.VMEM)
    hbm = pl.BlockSpec(memory_space=pltpu.HBM)
    return pl.pallas_call(
        finish_kernel,
        out_shape=(
            pltpu.HBM((rows, cols), jnp.float32),
            pltpu.HBM((rows, cols), jnp.float32),
            pltpu.HBM(absmax.shape, jnp.float32),
        ),
        in_specs=[vmem] * 5,
        out_specs=(hbm, hbm, hbm),
        scratch_shapes=[
            pltpu.VMEM((rows, cols), jnp.float32),
            pltpu.VMEM((rows, cols), jnp.float32),
            pltpu.SemaphoreType.DMA((2, tiles)),
            pltpu.SemaphoreType.DMA(()),
        ],
        compiler_params=pltpu.CompilerParams(vmem_limit_bytes=16 * 2**20),
        cost_estimate=pl.CostEstimate(
            flops=6 * rows * cols, bytes_accessed=18 * rows * cols, transcendentals=0
        ),
    )(factor, outer_params, gradient, momentum, absmax)


def per_device(outer_params, local_params, momentum):
    outer, gradient, momentum, absmax, factor = exchange(outer_params, local_params, momentum)
    return finish(factor, outer, gradient, momentum, absmax)


def solution(mesh):
    return jax.shard_map(
        per_device,
        mesh=mesh,
        in_specs=(P("shard", None), P("replica", "shard", None), P("shard", None)),
        out_specs=(P("shard", None), P("shard", None), P(None, "shard")),
        check_vma=False,
    )
```

time: 55.4 us -> 39.1 us (0.71)
  Pallas kernels: 54.6 us -> 38.3 us
    pallas_call x1, Pallas kernels: 52.3 us -> 36.1 us  [exchange(): pl.pallas_call(functools.partial(exchange_kernel, workers, shards, rows *...]
where the time goes in v2:
time: 39.1 us; the launch traced here: 38.9 us
  Pallas kernels  38.3 us (98%)
  between operations  0.64 us (2%)
    pallas_call x1, Pallas kernels, exchange(): pl.pallas_call(functools.partial(exchange_kernel, workers, shards, rows *...  36.1 us
    pallas_call x1, Pallas kernels, finish(): pl.pallas_call(finish_kernel, out_shape=(pltpu.HBM((rows, cols), jnp.floa...  2.23 us

profile of v2, /device:TPU:0, one launch (start us, length us, event | category | flops | bytes accessed | tf_op | source)
XLA Modules:
  0.0 38.9 jit_solution(8413215389402624872)
XLA Ops:
  0.6 36.1 %shard_map.58 = (f32[128,4096]{1,0:T(8,128)S(1)}, f32[128,4096]{1,0:T(8,128)S(1)}, f32[128,4096]{1,0:T(8,128)S(1)}, f32[32,128]{1,0:T(8,128)S(1)}, f32[8,128]{1,0:T(8,128)S(1)}) custom-call(f32[128,4096]{1,0:T(8,128)} %outer_hbm.1, bf16[1,128,4096]{2,1,0:T(8,128)(2,1)} %local_hbm.1, f32[128,4096]{1,0:T(8,128)} %momentum_hbm.1), custom_call_target="tpu_custom_call" | custom-call | flops 26214400 | bytes 16777216 | tf_op jit(solution)/shard_map/pallas_call | solution.py:390
  36.7 2.2 %shard_map.59 = (f32[128,4096]{1,0:T(8,128)}, f32[128,4096]{1,0:T(8,128)}, f32[32,128]{1,0:T(8,128)}) custom-call(f32[8,128]{1,0:T(8,128)S(1)} %get-tuple-element.8.factor_ref, f32[128,4096]{1,0:T(8,128)S(1)} %get-tuple-element.9.outer_ref, f32[128,4096]{1,0:T(8,128)S(1)} %get-tuple-element.10.gradient_ref, f32[128,4096]{1,0:T(8,128)S(1)} %get-tuple-element.11.momentum_ref, ...), custom_call_target="tpu_custom_call" | custom-call | flops 3145728 | bytes 9437184 | tf_op jit(solution)/shard_map/pallas_call | solution.py:475

commit v3 on v2

--- a/solution.py
+++ b/solution.py
@@ -20,11 +20,17 @@
 SHIFT = 1.5 * 2.0**23
 SQUARE = 4
 CODE_RANGE = 112.0
-SPLIT = (1, 2, 2, 2, 1)
-DIRECT = 1
-PIECES = 8
+SPLIT = (1, 1, 2, 2, 1, 1)
+DIRECT = 3
+WHOLE = 0
+EARLY = (4.1, 5.6, 0.7)
+PIECES = 4
+TILE = 16
+LANES = 1
+BEFORE = 8
+HALF = 8
 AHEAD = 3
-TURN = {"encode": 0.0, "quad": 2.2, "finish": 5.75, "pass": 6.8, "sent": 7.0, "decode": 7.1}
+TURN = {"encode": 0.0, "quad": 2.2, "finish": 4.75, "pass": 6.8, "sent": 7.0, "decode": 7.1}
 FILL = (1.6, 5.3, 5.35)
 
 
@@ -58,9 +64,9 @@
 def exchange_kernel(
     workers, shards, entry_count,
     outer_hbm, local_hbm, momentum_hbm, outer_v, gradient_out, momentum_out, max_out, factor_out,
-    local_v, raw, local_max, max_slots, inverse, spread, pair_own, pair_out, pair_in, quads,
+    local_v, raw, raw_whole, local_max, packed_max, max_slots, inverse, spread, pair_own, pair_out, pair_in, quads,
     gathered, squares,
-    load_sem, raw_send, raw_recv, max_send, max_recv, top_send, top_recv, pair_send, pair_recv,
+    load_sem, whole_send, whole_recv, raw_send, raw_recv, max_send, max_recv, top_send, top_recv, pair_send, pair_recv,
     quad_send, quad_recv, line_send, line_recv, pass_send, pass_recv, sq_send, sq_recv, momentum_sem,
 ):
     me = lax.axis_index("replica")
@@ -95,7 +101,7 @@
         return in_square(pick(kind, across, beside))
 
     def group_of(kind, place):
-        return kind * 2 + pick(kind, lax.rem(place, 2), place // 2)
+        return kind * 2 + pick(kind, place % 2 if isinstance(place, int) else lax.rem(place, 2), place // 2)
 
     def half_of(kind, place):
         return pick(kind, place // 2, lax.rem(place, 2))
@@ -107,7 +113,7 @@
         return slice(starts[part], starts[part + 1])
 
     def group_rows(group):
-        return pl.ds(pl.multiple_of(group * group_blocks, group_blocks), group_blocks)
+        return pl.ds(group * group_blocks if isinstance(group, int) else pl.multiple_of(group * group_blocks, group_blocks), group_blocks)
 
     def place_of(kind, place):
         return group_of(kind, place) * quarter + half_of(kind, place) * eighth
@@ -164,29 +170,70 @@
             raw_send, raw_recv.at[kind, part], first_mate(kind),
         )
 
+    def whole_copy(kind, part, mate):
+        return remote(
+            local_v.at[rows_of(part), span(place_of(kind, mates[mate]), eighth)], raw_whole.at[mate, kind, rows_of(part)],
+            whole_send, whole_recv.at[part], in_square(mates[mate]),
+        )
+
     per_piece = piece // BLOCK
-    for i in range(pieces):
-        for copy in loads(i):
-            copy.wait()
-
+    wide = lax.broadcasted_iota(jnp.int32, (rows, BLOCK), 1)
+
+    def piece_lanes(i, found):
+        for j in range(per_piece):
+            block = i * per_piece + j
+            at = slice(block * BLOCK, (block + 1) * BLOCK)
+            deltas = outer_v[:, at] - local_v[:, at].astype(jnp.float32)
+            found = jnp.where(wide == block, jnp.max(jnp.abs(deltas), axis=1, keepdims=True), found)
+        return found
+
+    def piece_max(i):
         for j in range(per_piece):
             block = i * per_piece + j
             at = slice(block * BLOCK, (block + 1) * BLOCK)
             deltas = outer_v[:, at] - local_v[:, at].astype(jnp.float32)
             local_max[block : block + 1, :] = jnp.max(jnp.abs(deltas).T, axis=0, keepdims=True)
 
+    found = jnp.zeros((rows, BLOCK), jnp.float32)
+    for i in range(pieces):
+        for copy in loads(i):
+            copy.wait()
+        if LANES:
+            found = piece_lanes(i, found)
+        else:
+            piece_max(i)
+    if LANES:
+        local_max[...] = found.T[: cols // BLOCK]
+
+    for place in range(SQUARE):
+        for kind in range(2):
+            packed_max[place, kind] = local_max[group_rows(group_of(kind, place))]
+
     pl.semaphore_wait(barrier, workers - 1 + len(beyond))
 
-    for step in range(workers - 1, 0, -1):
-        for kind in range(2):
-            remote(
-                local_max.at[group_rows(group_of(kind, lax.rem(peer(step), SQUARE)))], max_slots.at[step, kind],
-                max_send, max_recv, {"replica": peer(step)},
-            ).start()
+    def max_send_to(step, place):
+        slot = lax.rem(step * SQUARE + lax.rem(place + SQUARE - position, SQUARE), workers)
+        remote(
+            packed_max.at[place], max_slots.at[slot], max_send, max_recv,
+            {"replica": square_at(step) * SQUARE + place},
+        ).start()
+
+    for step in range(count - 1, -1, -1):
+        for place in (diagonal, across, beside, position):
+            if step > 0 or place is not position:
+                max_send_to(step, place)
+
+    def whole(part):
+        return part < WHOLE
 
     def raw_start(part):
-        for kind in range(2):
-            raw_copy(kind, part).start()
+        if whole(part):
+            for mate in range(3):
+                for kind in range(2):
+                    whole_copy(kind, part, mate).start()
+        else:
+            for kind in range(2):
+                raw_copy(kind, part).start()
 
     ahead = min(AHEAD, parts)
     for part in range(ahead):
@@ -244,6 +291,27 @@
             pair_out.at[kind, rows_of(part)], pair_in.at[kind, rows_of(part)],
             pair_send, pair_recv.at[kind, part], second_mate(kind),
         )
+
+    def whole_part(part):
+        wait_bytes(raw_whole.at[:, :, rows_of(part)], whole_recv.at[part])
+        for kind in range(2):
+            mine = half_of(kind, position) * eighth
+            for i in range(half_blocks):
+                at_rows = rows_of(part)
+                here = slice(i * BLOCK, (i + 1) * BLOCK)
+                at = span(place_of(kind, position) + i * BLOCK, BLOCK)
+                outer = outer_v[at_rows, at]
+                inv = inverse[kind, at_rows, span(mine + i * BLOCK, BLOCK)]
+                total = encode(outer - local_v[at_rows, at].astype(jnp.float32), inv)
+                for mate in range(3):
+                    total = total + encode(outer - raw_whole[mate, kind, at_rows, here].astype(jnp.float32), inv)
+                quads[my_square, kind, at_rows, here] = pack(total, most[1])
+            quad_start(kind, part)
+
+    def quad_start(kind, part):
+        for step in range(1, count):
+            slot = quads.at[my_square, kind, rows_of(part)]
+            remote(slot, slot, quad_send, quad_recv.at[part, step - 1], in_line(step)).start()
 
     def encode_part(kind, part):
         raw_copy(kind, part).wait_recv()
@@ -262,9 +330,7 @@
         pair_copy(kind, part).wait_recv()
         at = (kind, rows_of(part))
         quads[my_square, kind, rows_of(part)] = pack(pair_own[at] + unpack(pair_in[at], most[0]), most[1])
-        for step in range(1, count):
-            slot = quads.at[my_square, kind, rows_of(part)]
-            remote(slot, slot, quad_send, quad_recv.at[part, step], in_line(step)).start()
+        quad_start(kind, part)
 
     def line_copy(part):
         slot = gathered.at[position, :, rows_of(part)]
@@ -283,7 +349,7 @@
 
     def finish_part(part):
         for step in range(1, count):
-            wait_bytes(quads.at[square_from(step), :, rows_of(part)], quad_recv.at[part, step])
+            wait_bytes(quads.at[square_from(step), :, rows_of(part)], quad_recv.at[part, step - 1])
 
         at_rows = rows_of(part)
         square = squares[mine]
@@ -330,26 +396,34 @@
             remote(squares.at[mine], squares.at[mine], sq_send, sq_recv, device).start()
 
     def sent_all():
-        wait_bytes(raw, raw_send)
+        split_rows = pl.ds(starts[WHOLE], rows - starts[WHOLE])
+        whole_rows = pl.ds(0, starts[WHOLE])
+        if WHOLE > 0:
+            wait_bytes(raw_whole.at[:, :, whole_rows], whole_send)
+        wait_bytes(raw.at[:, split_rows], raw_send)
         wait_bytes(arrived, max_send)
         wait_bytes(max_slots.at[0], top_send)
-        wait_bytes(pair_out, pair_send)
+        wait_bytes(pair_out.at[:, split_rows], pair_send)
         wait_bytes(quads.at[pl.ds(0, count - 1)], quad_send)
         momentum_copy.wait()
 
     stages = []
     last = parts - 1
     for part in range(parts):
-        for kind in range(2):
+        if whole(part):
+            stages.append((part * 0.1 + 0.45, whole_part, (part,)))
+        for kind in range(0 if whole(part) else 2):
             stages.append((part + TURN["encode"] + 0.5 * kind, encode_part, (kind, part)))
             stages.append((part + TURN["quad"] + 0.5 * kind, quad_part, (kind, part)))
         if part + ahead < parts:
             stages.append((part + TURN["encode"] + 0.55, raw_start, (part + ahead,)))
-        stages.append((part + TURN["finish"], finish_part, (part,)))
+        finish = EARLY[0] + part * EARLY[2] if whole(part) else part + TURN["finish"]
+        stages.append((finish, finish_part, (part,)))
         if part == last:
-            stages.append((part + TURN["finish"], squares_start, ()))
-        stages.append((part + TURN["finish"], gather_part, (part,)))
-        stages.append((part + TURN["pass"], pass_part, (part,)))
+            stages.append((finish, squares_start, ()))
+        stages.append((finish, gather_part, (part,)))
+        passing = EARLY[1] + part * EARLY[2] if whole(part) else part + TURN["pass"]
+        stages.append((passing, pass_part, (part,)))
         stages.append((part * 0.01 + last + TURN["decode"], decode_line, (part,)))
         stages.append((part * 0.01 + last + TURN["decode"] + 0.05, decode_part, (part,)))
     for kind in range(2):
@@ -401,7 +475,9 @@
         scratch_shapes=[
             pltpu.VMEM((rows, cols), jnp.bfloat16),
             pltpu.VMEM((2, rows, quarter), jnp.bfloat16),
+            pltpu.VMEM((3, 2, rows, eighth), jnp.bfloat16),
             pltpu.VMEM((blocks, rows), jnp.float32),
+            pltpu.VMEM((SQUARE, 2, blocks // 4, rows), jnp.float32),
             pltpu.VMEM((workers, 2, blocks // 4, rows), jnp.float32),
             pltpu.VMEM((2, rows, quarter), jnp.float32),
             pltpu.VMEM((rows, cols), jnp.float32),
@@ -412,11 +488,12 @@
             pltpu.VMEM((SQUARE, 2, rows, eighth), jnp.bfloat16),
             pltpu.VMEM((SQUARE * shards, 8, BLOCK), jnp.float32),
             dma((2, PIECES)),
+            dma(()), dma((max(WHOLE, 1),)),
             dma(()), dma((2, parts)),
             dma(()), dma(()),
             dma(()), dma(()),
             dma(()), dma((2, parts)),
-            dma(()), dma((parts, count)),
+            dma(()), dma((parts, count - 1)),
             dma(()), dma((parts,)),
             dma(()), dma((parts, 2)),
             dma(()), dma(()),
@@ -469,7 +546,7 @@
 
 def finish(factor, outer_params, gradient, momentum, absmax):
     rows, cols = outer_params.shape
-    tiles = rows // 16
+    tiles = rows // TILE
     vmem = pl.BlockSpec(memory_space=pltpu.VMEM)
     hbm = pl.BlockSpec(memory_space=pltpu.HBM)
     return pl.pallas_call(

time: 39.1 us -> 37.4 us (0.957)
  Pallas kernels: 38.3 us -> 36.7 us
    pallas_call x1, Pallas kernels: 36.1 us -> 34.4 us  [exchange(): pl.pallas_call(functools.partial(exchange_kernel, workers, shards, rows *...]
where the time goes in v3:
time: 37.4 us; the launch traced here: 37.3 us
  Pallas kernels  36.7 us (98%)
  between operations  0.64 us (2%)
    pallas_call x1, Pallas kernels, exchange(): pl.pallas_call(functools.partial(exchange_kernel, workers, shards, rows *...  34.4 us
    pallas_call x1, Pallas kernels, finish(): pl.pallas_call(finish_kernel, out_shape=(pltpu.HBM((rows, cols), jnp.floa...  2.23 us

profile of v3, /device:TPU:0, one launch (start us, length us, event | category | flops | bytes accessed | tf_op | source)
XLA Modules:
  0.0 37.3 jit_solution(474490586652362737)
XLA Ops:
  0.6 34.4 %shard_map.58 = (f32[128,4096]{1,0:T(8,128)S(1)}, f32[128,4096]{1,0:T(8,128)S(1)}, f32[128,4096]{1,0:T(8,128)S(1)}, f32[32,128]{1,0:T(8,128)S(1)}, f32[8,128]{1,0:T(8,128)S(1)}) custom-call(f32[128,4096]{1,0:T(8,128)} %outer_hbm.1, bf16[1,128,4096]{2,1,0:T(8,128)(2,1)} %local_hbm.1, f32[128,4096]{1,0:T(8,128)} %momentum_hbm.1), custom_call_target="tpu_custom_call" | custom-call | flops 26214400 | bytes 16777216 | tf_op jit(solution)/shard_map/pallas_call | solution.py:464
  35.1 2.2 %shard_map.59 = (f32[128,4096]{1,0:T(8,128)}, f32[128,4096]{1,0:T(8,128)}, f32[32,128]{1,0:T(8,128)}) custom-call(f32[8,128]{1,0:T(8,128)S(1)} %get-tuple-element.8.factor_ref, f32[128,4096]{1,0:T(8,128)S(1)} %get-tuple-element.9.outer_ref, f32[128,4096]{1,0:T(8,128)S(1)} %get-tuple-element.10.gradient_ref, f32[128,4096]{1,0:T(8,128)S(1)} %get-tuple-element.11.momentum_ref, ...), custom_call_target="tpu_custom_call" | custom-call | flops 3145728 | bytes 9437184 | tf_op jit(solution)/shard_map/pallas_call | solution.py:552

commit v4 on v2

--- a/solution.py
+++ b/solution.py
@@ -20,11 +20,14 @@
 SHIFT = 1.5 * 2.0**23
 SQUARE = 4
 CODE_RANGE = 112.0
-SPLIT = (1, 2, 2, 2, 1)
-DIRECT = 1
-PIECES = 8
+SPLIT = (1, 1, 2, 2, 1, 1)
+DIRECT = 3
+HOLD = 1
+NEXT = 0.95
+PIECES = 4
+TILE = 16
 AHEAD = 3
-TURN = {"encode": 0.0, "quad": 2.2, "finish": 5.75, "pass": 6.8, "sent": 7.0, "decode": 7.1}
+TURN = {"encode": 0.0, "quad": 2.2, "finish": 4.75, "pass": 6.8, "sent": 7.0, "decode": 7.1}
 FILL = (1.6, 5.3, 5.35)
 
 
@@ -58,7 +61,7 @@
 def exchange_kernel(
     workers, shards, entry_count,
     outer_hbm, local_hbm, momentum_hbm, outer_v, gradient_out, momentum_out, max_out, factor_out,
-    local_v, raw, local_max, max_slots, inverse, spread, pair_own, pair_out, pair_in, quads,
+    local_v, raw, local_max, packed_max, max_slots, inverse, spread, pair_own, pair_out, pair_in, quads,
     gathered, squares,
     load_sem, raw_send, raw_recv, max_send, max_recv, top_send, top_recv, pair_send, pair_recv,
     quad_send, quad_recv, line_send, line_recv, pass_send, pass_recv, sq_send, sq_recv, momentum_sem,
@@ -95,7 +98,7 @@
         return in_square(pick(kind, across, beside))
 
     def group_of(kind, place):
-        return kind * 2 + pick(kind, lax.rem(place, 2), place // 2)
+        return kind * 2 + pick(kind, place % 2 if isinstance(place, int) else lax.rem(place, 2), place // 2)
 
     def half_of(kind, place):
         return pick(kind, place // 2, lax.rem(place, 2))
@@ -107,7 +110,7 @@
         return slice(starts[part], starts[part + 1])
 
     def group_rows(group):
-        return pl.ds(pl.multiple_of(group * group_blocks, group_blocks), group_blocks)
+        return pl.ds(group * group_blocks if isinstance(group, int) else pl.multiple_of(group * group_blocks, group_blocks), group_blocks)
 
     def place_of(kind, place):
         return group_of(kind, place) * quarter + half_of(kind, place) * eighth
@@ -165,24 +168,40 @@
         )
 
     per_piece = piece // BLOCK
-    for i in range(pieces):
-        for copy in loads(i):
-            copy.wait()
-
+    wide = lax.broadcasted_iota(jnp.int32, (rows, BLOCK), 1)
+
+    def piece_lanes(i, found):
         for j in range(per_piece):
             block = i * per_piece + j
             at = slice(block * BLOCK, (block + 1) * BLOCK)
             deltas = outer_v[:, at] - local_v[:, at].astype(jnp.float32)
-            local_max[block : block + 1, :] = jnp.max(jnp.abs(deltas).T, axis=0, keepdims=True)
+            found = jnp.where(wide == block, jnp.max(jnp.abs(deltas), axis=1, keepdims=True), found)
+        return found
+
+    found = jnp.zeros((rows, BLOCK), jnp.float32)
+    for i in range(pieces):
+        for copy in loads(i):
+            copy.wait()
+        found = piece_lanes(i, found)
+    local_max[...] = found.T[: cols // BLOCK]
+
+    for place in range(SQUARE):
+        for kind in range(2):
+            packed_max[place, kind] = local_max[group_rows(group_of(kind, place))]
 
     pl.semaphore_wait(barrier, workers - 1 + len(beyond))
 
-    for step in range(workers - 1, 0, -1):
-        for kind in range(2):
-            remote(
-                local_max.at[group_rows(group_of(kind, lax.rem(peer(step), SQUARE)))], max_slots.at[step, kind],
-                max_send, max_recv, {"replica": peer(step)},
-            ).start()
+    def max_send_to(step, place):
+        slot = lax.rem(step * SQUARE + lax.rem(place + SQUARE - position, SQUARE), workers)
+        remote(
+            packed_max.at[place], max_slots.at[slot], max_send, max_recv,
+            {"replica": square_at(step) * SQUARE + place},
+        ).start()
+
+    for step in range(count - 1, -1, -1):
+        for place in (diagonal, across, beside, position):
+            if step > 0 or place is not position:
+                max_send_to(step, place)
 
     def raw_start(part):
         for kind in range(2):
@@ -244,6 +263,11 @@
             pair_out.at[kind, rows_of(part)], pair_in.at[kind, rows_of(part)],
             pair_send, pair_recv.at[kind, part], second_mate(kind),
         )
+
+    def quad_start(kind, part):
+        for step in range(1, count):
+            slot = quads.at[my_square, kind, rows_of(part)]
+            remote(slot, slot, quad_send, quad_recv.at[part, step - 1], in_line(step)).start()
 
     def encode_part(kind, part):
         raw_copy(kind, part).wait_recv()
@@ -262,9 +286,7 @@
         pair_copy(kind, part).wait_recv()
         at = (kind, rows_of(part))
         quads[my_square, kind, rows_of(part)] = pack(pair_own[at] + unpack(pair_in[at], most[0]), most[1])
-        for step in range(1, count):
-            slot = quads.at[my_square, kind, rows_of(part)]
-            remote(slot, slot, quad_send, quad_recv.at[part, step], in_line(step)).start()
+        quad_start(kind, part)
 
     def line_copy(part):
         slot = gathered.at[position, :, rows_of(part)]
@@ -283,7 +305,7 @@
 
     def finish_part(part):
         for step in range(1, count):
-            wait_bytes(quads.at[square_from(step), :, rows_of(part)], quad_recv.at[part, step])
+            wait_bytes(quads.at[square_from(step), :, rows_of(part)], quad_recv.at[part, step - 1])
 
         at_rows = rows_of(part)
         square = squares[mine]
@@ -344,11 +366,13 @@
             stages.append((part + TURN["encode"] + 0.5 * kind, encode_part, (kind, part)))
             stages.append((part + TURN["quad"] + 0.5 * kind, quad_part, (kind, part)))
         if part + ahead < parts:
-            stages.append((part + TURN["encode"] + 0.55, raw_start, (part + ahead,)))
-        stages.append((part + TURN["finish"], finish_part, (part,)))
+            stages.append((part + TURN["encode"] + NEXT, raw_start, (part + ahead,)))
+        finish = part + TURN["finish"]
+        stages.append((finish, finish_part, (part,)))
         if part == last:
-            stages.append((part + TURN["finish"], squares_start, ()))
-        stages.append((part + TURN["finish"], gather_part, (part,)))
+            stages.append((finish, squares_start, ()))
+        held = max(finish, last + TURN["finish"] + 0.01) if part + HOLD >= last else finish
+        stages.append((held, gather_part, (part,)))
         stages.append((part + TURN["pass"], pass_part, (part,)))
         stages.append((part * 0.01 + last + TURN["decode"], decode_line, (part,)))
         stages.append((part * 0.01 + last + TURN["decode"] + 0.05, decode_part, (part,)))
@@ -402,6 +426,7 @@
             pltpu.VMEM((rows, cols), jnp.bfloat16),
             pltpu.VMEM((2, rows, quarter), jnp.bfloat16),
             pltpu.VMEM((blocks, rows), jnp.float32),
+            pltpu.VMEM((SQUARE, 2, blocks // 4, rows), jnp.float32),
             pltpu.VMEM((workers, 2, blocks // 4, rows), jnp.float32),
             pltpu.VMEM((2, rows, quarter), jnp.float32),
             pltpu.VMEM((rows, cols), jnp.float32),
@@ -416,7 +441,7 @@
             dma(()), dma(()),
             dma(()), dma(()),
             dma(()), dma((2, parts)),
-            dma(()), dma((parts, count)),
+            dma(()), dma((parts, count - 1)),
             dma(()), dma((parts,)),
             dma(()), dma((parts, 2)),
             dma(()), dma(()),
@@ -469,7 +494,7 @@
 
 def finish(factor, outer_params, gradient, momentum, absmax):
     rows, cols = outer_params.shape
-    tiles = rows // 16
+    tiles = rows // TILE
     vmem = pl.BlockSpec(memory_space=pltpu.VMEM)
     hbm = pl.BlockSpec(memory_space=pltpu.HBM)
     return pl.pallas_call(

time: 39.1 us -> 36.9 us (0.944)
  Pallas kernels: 38.3 us -> 36.1 us
    pallas_call x1, Pallas kernels: 36.1 us -> 33.8 us  [exchange(): pl.pallas_call(functools.partial(exchange_kernel, workers, shards, rows *...]
where the time goes in v4:
time: 36.9 us; the launch traced here: 36.7 us
  Pallas kernels  36.1 us (98%)
  between operations  0.64 us (2%)
    pallas_call x1, Pallas kernels, exchange(): pl.pallas_call(functools.partial(exchange_kernel, workers, shards, rows *...  33.8 us
    pallas_call x1, Pallas kernels, finish(): pl.pallas_call(finish_kernel, out_shape=(pltpu.HBM((rows, cols), jnp.floa...  2.23 us

profile of v4, /device:TPU:0, one launch (start us, length us, event | category | flops | bytes accessed | tf_op | source)
XLA Modules:
  0.0 36.7 jit_solution(13640642691109997608)
XLA Ops:
  0.6 33.8 %shard_map.58 = (f32[128,4096]{1,0:T(8,128)S(1)}, f32[128,4096]{1,0:T(8,128)S(1)}, f32[128,4096]{1,0:T(8,128)S(1)}, f32[32,128]{1,0:T(8,128)S(1)}, f32[8,128]{1,0:T(8,128)S(1)}) custom-call(f32[128,4096]{1,0:T(8,128)} %outer_hbm.1, bf16[1,128,4096]{2,1,0:T(8,128)(2,1)} %local_hbm.1, f32[128,4096]{1,0:T(8,128)} %momentum_hbm.1), custom_call_target="tpu_custom_call" | custom-call | flops 26214400 | bytes 16777216 | tf_op jit(solution)/shard_map/pallas_call | solution.py:414
  34.5 2.2 %shard_map.59 = (f32[128,4096]{1,0:T(8,128)}, f32[128,4096]{1,0:T(8,128)}, f32[32,128]{1,0:T(8,128)}) custom-call(f32[8,128]{1,0:T(8,128)S(1)} %get-tuple-element.8.factor_ref, f32[128,4096]{1,0:T(8,128)S(1)} %get-tuple-element.9.outer_ref, f32[128,4096]{1,0:T(8,128)S(1)} %get-tuple-element.10.gradient_ref, f32[128,4096]{1,0:T(8,128)S(1)} %get-tuple-element.11.momentum_ref, ...), custom_call_target="tpu_custom_call" | custom-call | flops 3145728 | bytes 9437184 | tf_op jit(solution)/shard_map/pallas_call | solution.py:500

commit v5 on v4

--- a/solution.py
+++ b/solution.py
@@ -27,7 +27,7 @@
 PIECES = 4
 TILE = 16
 AHEAD = 3
-TURN = {"encode": 0.0, "quad": 2.2, "finish": 4.75, "pass": 6.8, "sent": 7.0, "decode": 7.1}
+TURN = {"encode": 0.0, "quad": 2.2, "finish": 4.75, "pass": 7.1, "sent": 8.0, "decode": 8.1}
 FILL = (1.6, 5.3, 5.35)
 
 
@@ -204,7 +204,7 @@
                 max_send_to(step, place)
 
     def raw_start(part):
-        for kind in range(2):
+        for kind in (1, 0):
             raw_copy(kind, part).start()
 
     ahead = min(AHEAD, parts)

time: 36.9 us -> 36.9 us (level)
  no operation moved by 1% of the time
where the time goes in v5:
time: 36.9 us; the launch traced here: 36.7 us
  Pallas kernels  36.1 us (98%)
  between operations  0.64 us (2%)
    pallas_call x1, Pallas kernels, exchange(): pl.pallas_call(functools.partial(exchange_kernel, workers, shards, rows *...  33.8 us
    pallas_call x1, Pallas kernels, finish(): pl.pallas_call(finish_kernel, out_shape=(pltpu.HBM((rows, cols), jnp.floa...  2.23 us

profile of v5, /device:TPU:0, one launch (start us, length us, event | category | flops | bytes accessed | tf_op | source)
XLA Modules:
  0.0 36.7 jit_solution(10019583098954595643)
XLA Ops:
  0.6 33.8 %shard_map.58 = (f32[128,4096]{1,0:T(8,128)S(1)}, f32[128,4096]{1,0:T(8,128)S(1)}, f32[128,4096]{1,0:T(8,128)S(1)}, f32[32,128]{1,0:T(8,128)S(1)}, f32[8,128]{1,0:T(8,128)S(1)}) custom-call(f32[128,4096]{1,0:T(8,128)} %outer_hbm.1, bf16[1,128,4096]{2,1,0:T(8,128)(2,1)} %local_hbm.1, f32[128,4096]{1,0:T(8,128)} %momentum_hbm.1), custom_call_target="tpu_custom_call" | custom-call | flops 26214400 | bytes 16777216 | tf_op jit(solution)/shard_map/pallas_call | solution.py:414
  34.5 2.2 %shard_map.59 = (f32[128,4096]{1,0:T(8,128)}, f32[128,4096]{1,0:T(8,128)}, f32[32,128]{1,0:T(8,128)}) custom-call(f32[8,128]{1,0:T(8,128)S(1)} %get-tuple-element.8.factor_ref, f32[128,4096]{1,0:T(8,128)S(1)} %get-tuple-element.9.outer_ref, f32[128,4096]{1,0:T(8,128)S(1)} %get-tuple-element.10.gradient_ref, f32[128,4096]{1,0:T(8,128)S(1)} %get-tuple-element.11.momentum_ref, ...), custom_call_target="tpu_custom_call" | custom-call | flops 3145728 | bytes 9437184 | tf_op jit(solution)/shard_map/pallas_call | solution.py:500
